TPU v7x, 256 devices: a whole 4x4x8 slice. The times are simulated.
256 devices in a mesh: rep: 1, dp: 256 (over x, y, z, core).
Axes of the slice: x: 4, y: 4, z: 8, core: 2. Of those that a mesh axis runs over, the one named last changes fastest.
Arguments:
- a: bfloat16 [256, 2, 2048, 1024], P(('rep', 'dp'))
- g: bfloat16 [256, 2, 2048, 2816], P(('rep', 'dp'))
Outputs:
- output: bfloat16 [2, 1024, 2816], P('rep')
All inputs are finite; a program needn't handle non-finite values.
Results may differ from a plain program's by a relative error of at most 0.012.
Values are sent between devices in bfloat16 or wider.
A program may use at most 768 MiB of HBM per device.

v0:
```python
import jax
import jax.numpy as jnp


def solution(mesh):
    groups = mesh.shape["rep"]

    def step(a, g):
        a, g = (t.reshape(groups, -1, *t.shape[1:]) for t in (a, g))
        sums = jnp.einsum("rsntd,rsntf->rndf", a, g, preferred_element_type=jnp.float32)
        return sums.astype(jnp.bfloat16).reshape(-1, *sums.shape[2:])

    return step
```

profile of v0, /device:TPU:1, one launch (start us, length us, event | category | flops | bytes accessed | tf_op | source)
XLA Modules:
  0.0 257.5 jit_solution(14232209152890418178)
XLA Ops:
  0.0 33.5 %fusion = f32[2,1024,2816]{2,1,0:T(8,128)} fusion(bf16[1,2,2048,2816]{3,2,1,0:T(8,128)(2,1)} %param.1, bf16[1,2,2048,1024]{3,2,1,0:T(8,128)(2,1)} %param), kind=kOutput, calls=%fused_computation | convolution fusion | flops 23622320128 | bytes 54525952 | tf_op jit(solution)/rsntd,rsntf->rndf/dot_general | solution.py:10
  33.5 224.0 %all-reduce.2 = bf16[2,1024,2816]{2,1,0:T(8,128)(2,1)} all-reduce(f32[2,1024,2816]{2,1,0:T(8,128)} %fusion), channel_id=1, replica_groups=mesh['axis_0'=256] {'axis_0'}, use_global_device_ids=true, to_apply=%add.clone | all-reduce | flops 5767168 | bytes 34603008 | tf_op jit(solution)/rsntd,rsntf->rndf/dot_general | solution.py:10
where the time goes:
time: 258 us
  blocking collectives  224 us (87%)
  matrix products  33.5 us (13%)
    dot_general x1, blocking collectives, step(): jnp.einsum('rsntd,rsntf->rndf', a, g, preferred_element_type=jnp.float32)  224 us
    dot_general x1, matrix products, step(): jnp.einsum('rsntd,rsntf->rndf', a, g, preferred_element_type=jnp.float32)  33.5 us

commit v1 on v0

v1 whole, which is shorter than its diff:
```python
import jax
import jax.numpy as jnp
from jax import lax
from jax.experimental import pallas as pl
from jax.experimental.pallas import tpu as pltpu
from jax.sharding import PartitionSpec as P

BF16, F32 = jnp.bfloat16, jnp.float32
COLS = 256
LANES = 128
HALVE = {1: 3, 2: 5, 3: 7, 4: 9, 5: 11}
SWAP, SUM = 13, 16
GATHER = {4: 18, 3: 20, 2: 22, 1: 24, 0: 26}
DONE = 29


def kernel(
    blocks,
    a_ref,
    g_ref,
    out_ref,
    a_buf,
    g_buf,
    term,
    p_out,
    p_in,
    keep,
    st0, st1, st2, st3, st4, st5,
    rv0, rv1, rv2, rv3, rv4, rv5,
    x_out,
    x_in,
    a_sem,
    g_sem,
    p_send,
    p_recv,
    send,
    recv,
):
    stage, inbox = (st0, st1, st2, st3, st4, st5), (rv0, rv1, rv2, rv3, rv4, rv5)
    units = 2 * blocks
    rows = out_ref.shape[1]
    me = lax.axis_index("dp")
    core, z, y, x = me % 2, (me // 2) % 8, (me // 16) % 4, me // 64
    mate = me + 1 - 2 * core
    far = me + (((z + 4) % 8) - z) * 2

    def even(v):
        return 1 - 2 * (v % 2)

    def odd(v, n):
        return ((v + n - even(v)) % n) - v

    links = (
        me + 64 * even(x),
        me + 16 * even(y),
        me + 2 * even(z),
        me + 64 * odd(x, 4),
        me + 16 * odd(y, 4),
        me + 2 * odd(z, 8),
    )
    bits = (
        ((x + 1) // 2) % 2,
        ((y + 1) // 2) % 2,
        ((z + 1) // 2) % 2,
        (x // 2) % 2,
        (y // 2) % 2,
        (z // 2) % 2,
    )

    def pick(k, values):
        found = values[5]
        for i in range(5):
            found = jnp.where(k == i, values[i], found)
        return found

    def load_a(i):
        n = (core + 1 + i) % 2
        return pltpu.make_async_copy(a_ref.at[0, n], a_buf.at[i], a_sem.at[i])

    def load_g(i):
        own = jnp.where(i == 0, 0, (i + 1) % 2)
        own = jnp.where(i == 2 * blocks - 1, 1, own)
        block = jnp.where(own == 1, i // 2 - 1 + (i // (2 * blocks - 1)), (i + 1) // 2)
        n = (core + 1 + own) % 2
        col = pl.multiple_of(block * COLS, COLS)
        return pltpu.make_async_copy(
            g_ref.at[0, n, :, pl.ds(col, COLS)], g_buf.at[i % 4], g_sem.at[i % 4]
        )

    def multiply(i, which):
        load_g(i).wait()

        @pl.when(i + 3 < 2 * blocks)
        def _():
            load_g(i + 3).start()

        return lax.dot_general(
            a_buf[which],
            g_buf[i % 4],
            (((0,), (0,)), ((), ())),
            preferred_element_type=F32,
        )

    def push(src, dst, s_sem, r_sem, to):
        return pltpu.make_async_remote_copy(
            src_ref=src,
            dst_ref=dst,
            send_sem=s_sem,
            recv_sem=r_sem,
            device_id={"dp": to},
            device_id_type=pl.DeviceIdType.MESH,
        )

    def push_mate(b):
        return push(p_out.at[b], p_in.at[b], p_send.at[b], p_recv.at[b], mate)

    def push_half(u, s):
        return push(
            stage[s].at[u],
            inbox[s].at[u],
            send.at[s, u],
            recv.at[s, u],
            pick((u + s) % 6, links),
        )

    def push_far(u):
        return push(x_out.at[u], x_in.at[u], send.at[6, u], recv.at[6, u], far)

    def kept(u, s):
        begin = 0
        for k in range(s):
            begin = begin + pick((u + k) % 6, bits) * (rows >> (k + 1))
        return begin

    def push_rows(u, s, begin, to, slot):
        place = out_ref.at[
            core,
            pl.ds(pl.multiple_of(begin, 16), rows >> (s + 1)),
            pl.ds(pl.multiple_of(u * LANES, LANES), LANES),
        ]
        return push(place, place, send.at[slot, u], recv.at[slot, u], to)

    def push_gather(u, s):
        return push_rows(u, s, kept(u, s + 1), pick((u + s) % 6, links), 7 + s)

    def wait_gather(u, s):
        bit = pick((u + s) % 6, bits)
        begin = kept(u, s) + (1 - bit) * (rows >> (s + 1))
        push_rows(u, s, begin, pick((u + s) % 6, links), 7 + s).wait_recv()

    def push_done(u, owner):
        place = out_ref.at[owner, :, pl.ds(pl.multiple_of(u * LANES, LANES), LANES)]
        return push(place, place, send.at[13, u], recv.at[13, u], mate)

    def each(begin, count, size, fn):
        step = min(size, count)
        for i in range(count // step):
            fn(pl.ds(pl.multiple_of(begin + i * step, 16), step), pl.ds(i * step, step))

    for i in range(2):
        load_a(i).start()
    for i in range(3):
        load_g(i).start()

    barrier = pltpu.get_barrier_semaphore()
    for other in (*links, far, mate):
        pl.semaphore_signal(
            barrier,
            inc=1,
            device_id={"dp": other},
            device_id_type=pl.DeviceIdType.MESH,
        )

    def mate_block(b, i):
        p_out[b] = multiply(i, 0).astype(BF16)
        push_mate(b).start()

    load_a(0).wait()
    load_a(1).wait()
    pl.semaphore_wait(barrier, 8)
    mate_block(0, 0)

    def first_half(u, h):
        bit = pick(u % 6, bits)
        cols = slice(h * LANES, (h + 1) * LANES)
        half = rows // 2

        def to_send(src, dst):
            both = term[src, cols] + p_in[u // 2, src, cols].astype(F32)
            st0[u, dst, :] = both.astype(BF16)

        def to_keep(src, dst):
            keep[u, dst, :] = term[src, cols] + p_in[u // 2, src, cols].astype(F32)

        each((1 - bit) * half, half, 128, to_send)
        push_half(u, 0).start()
        each(bit * half, half, 128, to_keep)

    def halve(u, s):
        size = rows >> (s + 1)
        bit = pick((u + s) % 6, bits)
        base = kept(u, s) - kept(u, 1)
        push_half(u, s - 1).wait_recv()
        gone, stay = (1 - bit) * size, bit * size

        def at(begin, i, n):
            return pl.ds(pl.multiple_of(begin + i, 16), n)

        n = min(size, 128)
        for i in range(0, size, n):
            both = keep[u, at(base + gone, i, n), :] + inbox[s - 1][
                u, at(gone, i, n), :
            ].astype(F32)
            stage[s][u, pl.ds(i, n), :] = both.astype(BF16)
        push_half(u, s).start()
        for i in range(0, size, n):
            keep[u, at(base + stay, i, n), :] = keep[
                u, at(base + stay, i, n), :
            ] + inbox[s - 1][u, at(stay, i, n), :].astype(F32)

    def swap(u):
        push_half(u, 5).wait_recv()
        at = pl.ds(pl.multiple_of(kept(u, 6) - kept(u, 1), 16), 16)
        x_out[u] = (keep[u, at, :] + rv5[u].astype(F32)).astype(BF16)
        push_far(u).start()

    def total(u):
        push_far(u).wait_recv()
        both = (x_out[u].astype(F32) + x_in[u].astype(F32)).astype(BF16)
        at = pl.ds(pl.multiple_of(kept(u, 6), 16), 16)
        out_ref[core, at, pl.ds(pl.multiple_of(u * LANES, LANES), LANES)] = both
        push_gather(u, 5).start()

    def gather(u, s):
        wait_gather(u, s + 1)
        push_gather(u, s).start()

    def done(u):
        wait_gather(u, 0)
        push_done(u, core).start()

    def slot(t, _):
        @pl.when(t < blocks)
        def _():
            @pl.when(t + 1 < blocks)
            def _():
                mate_block(t + 1, 2 * t + 1)

            term[...] = multiply(jnp.where(t == blocks - 1, 2 * t + 1, 2 * t + 2), 1)
            push_mate(t).wait_recv()
            for h in range(2):
                first_half(2 * t + h, h)

        def late(delay, fn):
            b = t - delay

            @pl.when((b >= 0) & (b < blocks))
            def _():
                def one(h, _):
                    fn(2 * b + h)
                    return 0

                lax.fori_loop(0, 2, one, 0)

        late(DONE, done)
        for s in range(5):
            late(GATHER[s], lambda u, s=s: gather(u, s))
        late(SUM, total)
        late(SWAP, swap)
        for s in range(5, 0, -1):
            late(HALVE[s], lambda u, s=s: halve(u, s))
        return 0

    lax.fori_loop(0, blocks + DONE, slot, 0)

    def finish_block(b, _):
        push_mate(b).wait_send()
        return 0

    lax.fori_loop(0, blocks, finish_block, 0)

    def finish(u, _):
        for s in range(6):
            push_half(u, s).wait_send()
            push_gather(u, s).wait_send()
        push_far(u).wait_send()
        push_done(u, 1 - core).wait_recv()
        push_done(u, core).wait_send()
        return 0

    lax.fori_loop(0, units, finish, 0)


def solution(mesh):
    def step(a, g):
        (_, n, tokens, d), f = a.shape, g.shape[-1]
        blocks, units = f // COLS, f // LANES
        halves = [pltpu.VMEM((units, d >> (s + 1), LANES), BF16) for s in range(6)]
        dma = pltpu.SemaphoreType.DMA
        import functools

        return pl.pallas_call(
            functools.partial(kernel, blocks),
            out_shape=jax.ShapeDtypeStruct((n, d, f), BF16),
            in_specs=[pl.BlockSpec(memory_space=pl.ANY)] * 2,
            out_specs=pl.BlockSpec(memory_space=pltpu.VMEM),
            scratch_shapes=[
                pltpu.VMEM((2, tokens, d), BF16),
                pltpu.VMEM((4, tokens, COLS), BF16),
                pltpu.VMEM((d, COLS), F32),
                pltpu.VMEM((blocks, d, COLS), BF16),
                pltpu.VMEM((blocks, d, COLS), BF16),
                pltpu.VMEM((units, d // 2, LANES), F32),
                *halves,
                *halves,
                pltpu.VMEM((units, d >> 6, LANES), BF16),
                pltpu.VMEM((units, d >> 6, LANES), BF16),
                dma((2,)),
                dma((4,)),
                dma((blocks,)),
                dma((blocks,)),
                dma((14, units)),
                dma((14, units)),
            ],
            compiler_params=pltpu.CompilerParams(
                collective_id=0, has_side_effects=True, vmem_limit_bytes=62 * 2**20
            ),
            name="sums",
        )(a, g)

    return jax.shard_map(
        step,
        mesh=mesh,
        in_specs=(P(("rep", "dp")), P(("rep", "dp"))),
        out_specs=P("rep"),
        check_vma=False,
    )
```

time: 258 us -> 126 us (0.49)
  blocking collectives: 224 us -> 0 us
  Pallas kernels: 0 us -> 116 us
  matrix products: 33.5 us -> 0 us
  local copies, waits for them, and re-layouts: 0 us -> 9.87 us
    dot_general x1 -> x0, blocking collectives: 224 us -> none  [step(): jnp.einsum('rsntd,rsntf->rndf', a, g, preferred_element_type=jnp.float32)]
    pallas_call x0 -> x1, Pallas kernels: none -> 116 us  [step(): pl.pallas_call(functools.partial(kernel, blocks), out_shape=jax.ShapeDtyp...]
    dot_general x1 -> x0, matrix products: 33.5 us -> none  [step(): jnp.einsum('rsntd,rsntf->rndf', a, g, preferred_element_type=jnp.float32)]
    unnamed x0 -> x1, local copies, waits for them, and re-layouts: none -> 9.87 us
where the time goes in v1:
time: 126 us; the launch traced here: 125 us
  Pallas kernels  116 us (92%)
  local copies, waits for them, and re-layouts  9.87 us (8%)
    pallas_call x1, Pallas kernels, step(): pl.pallas_call(functools.partial(kernel, blocks), out_shape=jax.ShapeDtyp...  116 us
    unnamed x1, local copies, waits for them, and re-layouts  9.87 us

profile of v1, /device:TPU:1, one launch (start us, length us, event | category | flops | bytes accessed | tf_op | source)
XLA Modules:
  0.0 125.4 jit_solution(13999084438515070208)
XLA Ops:
  0.0 115.5 %sums.1 = bf16[2,1024,2816]{2,1,0:T(8,128)(2,1)} custom-call(bf16[1,2,2048,1024]{3,2,1,0:T(8,128)(2,1)} %a_ref.1, bf16[1,2,2048,2816]{3,2,1,0:T(8,128)(2,1)} %g_ref.1), custom_call_target="tpu_custom_call" | custom-call | tf_op jit(solution)/shard_map/sums/pallas_call | solution.py:302
  115.5 9.9 %copy.4 = bf16[2,1024,2816]{2,1,0:T(8,128)(2,1)} copy(bf16[2,1024,2816]{2,1,0:T(8,128)(2,1)} %sums.1) | data formatting | bytes 23068672

commit v2 on v1

--- a/solution.py
+++ b/solution.py
@@ -1,3 +1,5 @@
+import functools
+
 import jax
 import jax.numpy as jnp
 from jax import lax
@@ -8,10 +10,9 @@
 BF16, F32 = jnp.bfloat16, jnp.float32
 COLS = 256
 LANES = 128
-HALVE = {1: 3, 2: 5, 3: 7, 4: 9, 5: 11}
-SWAP, SUM = 13, 16
-GATHER = {4: 18, 3: 20, 2: 22, 1: 24, 0: 26}
-DONE = 29
+PIECE = 16
+HALVE1, HALVE2, SCATTER, SWAP, SUM = 5, 8, 11, 14, 18
+SPREAD, GATHER1, GATHER0, DONE = 21, 24, 27, 31
 
 
 def kernel(
@@ -25,8 +26,14 @@
     p_out,
     p_in,
     keep,
-    st0, st1, st2, st3, st4, st5,
-    rv0, rv1, rv2, rv3, rv4, rv5,
+    st0,
+    st1,
+    st2,
+    rv0,
+    rv1,
+    rv2,
+    cube_out,
+    cube_in,
     x_out,
     x_in,
     a_sem,
@@ -36,7 +43,7 @@
     send,
     recv,
 ):
-    stage, inbox = (st0, st1, st2, st3, st4, st5), (rv0, rv1, rv2, rv3, rv4, rv5)
+    stage, inbox = (st0, st1, st2), (rv0, rv1, rv2)
     units = 2 * blocks
     rows = out_ref.shape[1]
     me = lax.axis_index("dp")
@@ -67,7 +74,8 @@
         (z // 2) % 2,
     )
 
-    def pick(k, values):
+    def pick(u, s, values):
+        k = (u + 3 * core + s) % 6
         found = values[5]
         for i in range(5):
             found = jnp.where(k == i, values[i], found)
@@ -120,50 +128,81 @@
             inbox[s].at[u],
             send.at[s, u],
             recv.at[s, u],
-            pick((u + s) % 6, links),
+            pick(u, s, links),
         )
 
     def push_far(u):
-        return push(x_out.at[u], x_in.at[u], send.at[6, u], recv.at[6, u], far)
+        return push(x_out.at[u], x_in.at[u], send.at[4, u], recv.at[4, u], far)
+
+    def cube(u):
+        others = []
+        for m in range(1, 8):
+            piece, to = 0, me
+            for k in range(3):
+                bit = pick(u, 3 + k, bits)
+                if m >> k & 1:
+                    bit = 1 - bit
+                    to = to + pick(u, 3 + k, links) - me
+                piece = piece + bit * ((4 * PIECE) >> k)
+            others.append((m - 1, pl.multiple_of(piece, PIECE), to))
+        return others
+
+    def push_cube(u, m, piece, to):
+        return push(
+            cube_out.at[u, pl.ds(piece, PIECE)],
+            cube_in.at[u, m],
+            send.at[3, u],
+            recv.at[3, u],
+            to,
+        )
+
+    def all_cube(u, k):
+        return push(cube_in.at[u], cube_in.at[u], send.at[k, u], recv.at[k, u], far)
 
     def kept(u, s):
         begin = 0
         for k in range(s):
-            begin = begin + pick((u + k) % 6, bits) * (rows >> (k + 1))
+            begin = begin + pick(u, k, bits) * (rows >> (k + 1))
         return begin
 
-    def push_rows(u, s, begin, to, slot):
+    def push_rows(u, begin, size, to, k):
         place = out_ref.at[
             core,
-            pl.ds(pl.multiple_of(begin, 16), rows >> (s + 1)),
+            pl.ds(pl.multiple_of(begin, PIECE), size),
             pl.ds(pl.multiple_of(u * LANES, LANES), LANES),
         ]
-        return push(place, place, send.at[slot, u], recv.at[slot, u], to)
+        return push(place, place, send.at[k, u], recv.at[k, u], to)
 
     def push_gather(u, s):
-        return push_rows(u, s, kept(u, s + 1), pick((u + s) % 6, links), 7 + s)
+        return push_rows(u, kept(u, s + 1), rows >> (s + 1), pick(u, s, links), 6 + s)
 
     def wait_gather(u, s):
-        bit = pick((u + s) % 6, bits)
-        begin = kept(u, s) + (1 - bit) * (rows >> (s + 1))
-        push_rows(u, s, begin, pick((u + s) % 6, links), 7 + s).wait_recv()
+        begin = kept(u, s) + (1 - pick(u, s, bits)) * (rows >> (s + 1))
+        push_rows(u, begin, rows >> (s + 1), pick(u, s, links), 6 + s).wait_recv()
 
     def push_done(u, owner):
         place = out_ref.at[owner, :, pl.ds(pl.multiple_of(u * LANES, LANES), LANES)]
-        return push(place, place, send.at[13, u], recv.at[13, u], mate)
+        return push(place, place, send.at[9, u], recv.at[9, u], mate)
 
     def each(begin, count, size, fn):
         step = min(size, count)
         for i in range(count // step):
             fn(pl.ds(pl.multiple_of(begin + i * step, 16), step), pl.ds(i * step, step))
 
-    for i in range(2):
-        load_a(i).start()
-    for i in range(3):
-        load_g(i).start()
+    load_a(0).start()
+    load_g(0).start()
+    load_g(1).start()
 
     barrier = pltpu.get_barrier_semaphore()
-    for other in (*links, far, mate):
+    peers = sorted(
+        {
+            tuple(sorted((r + 3 + k) % 6 for k in range(3) if m >> k & 1))
+            for r in range(6)
+            for m in range(1, 8)
+        }
+    )
+    others = [me + sum(links[k] - me for k in peer) for peer in peers] + [far, mate]
+    for other in others:
         pl.semaphore_signal(
             barrier,
             inc=1,
@@ -176,12 +215,14 @@
         push_mate(b).start()
 
     load_a(0).wait()
-    load_a(1).wait()
-    pl.semaphore_wait(barrier, 8)
-    mate_block(0, 0)
+    load_a(1).start()
+    load_g(2).start()
+    p_out[0] = multiply(0, 0).astype(BF16)
+    pl.semaphore_wait(barrier, len(others))
+    push_mate(0).start()
 
     def first_half(u, h):
-        bit = pick(u % 6, bits)
+        bit = pick(u, 0, bits)
         cols = slice(h * LANES, (h + 1) * LANES)
         half = rows // 2
 
@@ -198,7 +239,7 @@
 
     def halve(u, s):
         size = rows >> (s + 1)
-        bit = pick((u + s) % 6, bits)
+        bit = pick(u, s, bits)
         base = kept(u, s) - kept(u, 1)
         push_half(u, s - 1).wait_recv()
         gone, stay = (1 - bit) * size, bit * size
@@ -218,18 +259,36 @@
                 u, at(base + stay, i, n), :
             ] + inbox[s - 1][u, at(stay, i, n), :].astype(F32)
 
+    def scatter(u):
+        push_half(u, 2).wait_recv()
+        base = kept(u, 3) - kept(u, 1)
+        at = pl.ds(pl.multiple_of(base, PIECE), 8 * PIECE)
+        both = keep[u, at, :] + rv2[u].astype(F32)
+        cube_out[u] = both.astype(BF16)
+        for m, piece, to in cube(u):
+            push_cube(u, m, piece, to).start()
+        keep[u, at, :] = both
+
     def swap(u):
-        push_half(u, 5).wait_recv()
-        at = pl.ds(pl.multiple_of(kept(u, 6) - kept(u, 1), 16), 16)
-        x_out[u] = (keep[u, at, :] + rv5[u].astype(F32)).astype(BF16)
+        all_cube(u, 3).wait_recv()
+        both = keep[u, pl.ds(pl.multiple_of(kept(u, 6) - kept(u, 1), PIECE), PIECE), :]
+        for m in range(7):
+            both = both + cube_in[u, m].astype(F32)
+        x_out[u] = both.astype(BF16)
         push_far(u).start()
 
     def total(u):
         push_far(u).wait_recv()
         both = (x_out[u].astype(F32) + x_in[u].astype(F32)).astype(BF16)
-        at = pl.ds(pl.multiple_of(kept(u, 6), 16), 16)
+        begin = kept(u, 6)
+        at = pl.ds(pl.multiple_of(begin, PIECE), PIECE)
         out_ref[core, at, pl.ds(pl.multiple_of(u * LANES, LANES), LANES)] = both
-        push_gather(u, 5).start()
+        for _, _, to in cube(u):
+            push_rows(u, begin, PIECE, to, 5).start()
+
+    def spread(u):
+        all_cube(u, 5).wait_recv()
+        push_gather(u, 2).start()
 
     def gather(u, s):
         wait_gather(u, s + 1)
@@ -239,39 +298,54 @@
         wait_gather(u, 0)
         push_done(u, core).start()
 
+    steps = (
+        (DONE, done),
+        (GATHER0, lambda u: gather(u, 0)),
+        (GATHER1, lambda u: gather(u, 1)),
+        (SPREAD, spread),
+        (SUM, total),
+        (SWAP, swap),
+        (SCATTER, scatter),
+        (HALVE2, lambda u: halve(u, 2)),
+        (HALVE1, lambda u: halve(u, 1)),
+    )
+
+    def tick(t, part):
+        for delay, fn in steps:
+            if delay % 2 != part:
+                continue
+            b = t - delay // 2
+
+            @pl.when((b >= 0) & (b < blocks))
+            def _(b=b, fn=fn):
+                def one(h, _):
+                    fn(2 * b + h)
+                    return 0
+
+                lax.fori_loop(0, 2, one, 0)
+
     def slot(t, _):
+        @pl.when(t + 1 < blocks)
+        def _():
+            mate_block(t + 1, 2 * t + 1)
+
+        tick(t, 0)
+
         @pl.when(t < blocks)
         def _():
-            @pl.when(t + 1 < blocks)
+            @pl.when(t == 0)
             def _():
-                mate_block(t + 1, 2 * t + 1)
+                load_a(1).wait()
 
             term[...] = multiply(jnp.where(t == blocks - 1, 2 * t + 1, 2 * t + 2), 1)
             push_mate(t).wait_recv()
             for h in range(2):
                 first_half(2 * t + h, h)
 
-        def late(delay, fn):
-            b = t - delay
-
-            @pl.when((b >= 0) & (b < blocks))
-            def _():
-                def one(h, _):
-                    fn(2 * b + h)
-                    return 0
-
-                lax.fori_loop(0, 2, one, 0)
-
-        late(DONE, done)
-        for s in range(5):
-            late(GATHER[s], lambda u, s=s: gather(u, s))
-        late(SUM, total)
-        late(SWAP, swap)
-        for s in range(5, 0, -1):
-            late(HALVE[s], lambda u, s=s: halve(u, s))
+        tick(t, 1)
         return 0
 
-    lax.fori_loop(0, blocks + DONE, slot, 0)
+    lax.fori_loop(0, blocks + DONE // 2, slot, 0)
 
     def finish_block(b, _):
         push_mate(b).wait_send()
@@ -280,9 +354,11 @@
     lax.fori_loop(0, blocks, finish_block, 0)
 
     def finish(u, _):
-        for s in range(6):
+        for s in range(3):
             push_half(u, s).wait_send()
             push_gather(u, s).wait_send()
+        all_cube(u, 3).wait_send()
+        all_cube(u, 5).wait_send()
         push_far(u).wait_send()
         push_done(u, 1 - core).wait_recv()
         push_done(u, core).wait_send()
@@ -291,17 +367,33 @@
     lax.fori_loop(0, units, finish, 0)
 
 
+def flush(sums_ref, out_ref, sem):
+    n, rows, _ = sums_ref.shape
+    step = rows // 4
+    copies = [
+        pltpu.make_async_copy(
+            sums_ref.at[i, pl.ds(j * step, step)],
+            out_ref.at[i, pl.ds(j * step, step)],
+            sem.at[i, j],
+        )
+        for i in range(n)
+        for j in range(4)
+    ]
+    for copy in copies:
+        copy.start()
+    for copy in copies:
+        copy.wait()
+
+
 def solution(mesh):
     def step(a, g):
         (_, n, tokens, d), f = a.shape, g.shape[-1]
         blocks, units = f // COLS, f // LANES
-        halves = [pltpu.VMEM((units, d >> (s + 1), LANES), BF16) for s in range(6)]
+        halves = [pltpu.VMEM((units, d >> (s + 1), LANES), BF16) for s in range(3)]
         dma = pltpu.SemaphoreType.DMA
-        import functools
-
-        return pl.pallas_call(
+        sums = pl.pallas_call(
             functools.partial(kernel, blocks),
-            out_shape=jax.ShapeDtypeStruct((n, d, f), BF16),
+            out_shape=pltpu.VMEM((n, d, f), BF16),
             in_specs=[pl.BlockSpec(memory_space=pl.ANY)] * 2,
             out_specs=pl.BlockSpec(memory_space=pltpu.VMEM),
             scratch_shapes=[
@@ -313,20 +405,31 @@
                 pltpu.VMEM((units, d // 2, LANES), F32),
                 *halves,
                 *halves,
-                pltpu.VMEM((units, d >> 6, LANES), BF16),
-                pltpu.VMEM((units, d >> 6, LANES), BF16),
+                pltpu.VMEM((units, 8 * PIECE, LANES), BF16),
+                pltpu.VMEM((units, 7, PIECE, LANES), BF16),
+                pltpu.VMEM((units, PIECE, LANES), BF16),
+                pltpu.VMEM((units, PIECE, LANES), BF16),
                 dma((2,)),
                 dma((4,)),
                 dma((blocks,)),
                 dma((blocks,)),
-                dma((14, units)),
-                dma((14, units)),
+                dma((10, units)),
+                dma((10, units)),
             ],
             compiler_params=pltpu.CompilerParams(
-                collective_id=0, has_side_effects=True, vmem_limit_bytes=62 * 2**20
+                collective_id=0, has_side_effects=True, vmem_limit_bytes=46 * 2**20
             ),
             name="sums",
         )(a, g)
+        return pl.pallas_call(
+            flush,
+            out_shape=jax.ShapeDtypeStruct((n, d, f), BF16),
+            in_specs=[pl.BlockSpec(memory_space=pltpu.VMEM)],
+            out_specs=pl.BlockSpec(memory_space=pl.ANY),
+            scratch_shapes=[dma((2, 4))],
+            compiler_params=pltpu.CompilerParams(vmem_limit_bytes=2**20),
+            name="flush",
+        )(sums)
 
     return jax.shard_map(
         step,

time: 126 us -> 105 us (0.83)
  Pallas kernels: 116 us -> 105 us
  local copies, waits for them, and re-layouts: 9.87 us -> 0 us
    pallas_call x1 -> x2, Pallas kernels: 116 us -> 105 us  [the longest x1 101 us: step(): pl.pallas_call(functools.partial(kernel, blocks), out_shape=pltpu.VMEM((n...]
    unnamed x1 -> x0, local copies, waits for them, and re-layouts: 9.87 us -> none
where the time goes in v2:
time: 105 us
  Pallas kernels  105 us (100%)
    pallas_call x1, Pallas kernels, step(): pl.pallas_call(functools.partial(kernel, blocks), out_shape=pltpu.VMEM((n...  101 us
    pallas_call x1, Pallas kernels, step(): pl.pallas_call(flush, out_shape=jax.ShapeDtypeStruct((n, d, f), BF16), in...  4.33 us

profile of v2, /device:TPU:1, one launch (start us, length us, event | category | flops | bytes accessed | tf_op | source)
XLA Modules:
  0.0 105.4 jit_solution(15189890095589428417)
XLA Ops:
  0.0 101.0 %sums.1.sums_ref = bf16[2,1024,2816]{2,1,0:T(8,128)(2,1)S(1)} custom-call(bf16[1,2,2048,1024]{3,2,1,0:T(8,128)(2,1)} %a_ref.1, bf16[1,2,2048,2816]{3,2,1,0:T(8,128)(2,1)} %g_ref.1), custom_call_target="tpu_custom_call" | custom-call | tf_op jit(solution)/shard_map/sums/pallas_call | solution.py:394
  101.0 4.3 %flush.1 = bf16[2,1024,2816]{2,1,0:T(8,128)(2,1)} custom-call(bf16[2,1024,2816]{2,1,0:T(8,128)(2,1)S(1)} %sums.1.sums_ref), custom_call_target="tpu_custom_call" | custom-call | tf_op jit(solution)/shard_map/flush/pallas_call | solution.py:424

commit v3 on v2

--- a/solution.py
+++ b/solution.py
@@ -11,8 +11,8 @@
 COLS = 256
 LANES = 128
 PIECE = 16
-HALVE1, HALVE2, SCATTER, SWAP, SUM = 5, 8, 11, 14, 18
-SPREAD, GATHER1, GATHER0, DONE = 21, 24, 27, 31
+HALVE1, HALVE2, SCATTER, SWAP, SUM = 4, 7, 11, 15, 21
+SPREAD, GATHER1, GATHER0, DONE = 26, 31, 37, 45
 
 
 def kernel(
@@ -42,9 +42,9 @@
     p_recv,
     send,
     recv,
+    done_recv,
 ):
     stage, inbox = (st0, st1, st2), (rv0, rv1, rv2)
-    units = 2 * blocks
     rows = out_ref.shape[1]
     me = lax.axis_index("dp")
     core, z, y, x = me % 2, (me // 2) % 8, (me // 16) % 4, me // 64
@@ -120,30 +120,30 @@
         )
 
     def push_mate(b):
-        return push(p_out.at[b], p_in.at[b], p_send.at[b], p_recv.at[b], mate)
+        return push(p_out.at[b], p_in.at[b], p_send, p_recv.at[b], mate)
 
     def push_half(u, s):
         return push(
             stage[s].at[u],
             inbox[s].at[u],
-            send.at[s, u],
+            send.at[s],
             recv.at[s, u],
             pick(u, s, links),
         )
 
     def push_far(u):
-        return push(x_out.at[u], x_in.at[u], send.at[4, u], recv.at[4, u], far)
+        return push(x_out.at[u], x_in.at[u], send.at[4], recv.at[4, u], far)
 
     def cube(u):
         others = []
+        bit = [pick(u, 3 + k, bits) for k in range(3)]
+        hop = [pick(u, 3 + k, links) - me for k in range(3)]
         for m in range(1, 8):
             piece, to = 0, me
             for k in range(3):
-                bit = pick(u, 3 + k, bits)
-                if m >> k & 1:
-                    bit = 1 - bit
-                    to = to + pick(u, 3 + k, links) - me
-                piece = piece + bit * ((4 * PIECE) >> k)
+                there = 1 - bit[k] if m >> k & 1 else bit[k]
+                piece = piece + there * ((4 * PIECE) >> k)
+                to = to + hop[k] if m >> k & 1 else to
             others.append((m - 1, pl.multiple_of(piece, PIECE), to))
         return others
 
@@ -151,13 +151,14 @@
         return push(
             cube_out.at[u, pl.ds(piece, PIECE)],
             cube_in.at[u, m],
-            send.at[3, u],
+            send.at[3],
             recv.at[3, u],
             to,
         )
 
-    def all_cube(u, k):
-        return push(cube_in.at[u], cube_in.at[u], send.at[k, u], recv.at[k, u], far)
+    def arrived(u, k):
+        buf = (rv0, rv1, rv2, cube_in, x_in, cube_in, rv2, rv1, rv0)[k]
+        push(buf.at[u], buf.at[u], send.at[k], recv.at[k, u], mate).wait_recv()
 
     def kept(u, s):
         begin = 0
@@ -171,18 +172,14 @@
             pl.ds(pl.multiple_of(begin, PIECE), size),
             pl.ds(pl.multiple_of(u * LANES, LANES), LANES),
         ]
-        return push(place, place, send.at[k, u], recv.at[k, u], to)
-
-    def push_gather(u, s):
-        return push_rows(u, kept(u, s + 1), rows >> (s + 1), pick(u, s, links), 6 + s)
-
-    def wait_gather(u, s):
-        begin = kept(u, s) + (1 - pick(u, s, bits)) * (rows >> (s + 1))
-        push_rows(u, begin, rows >> (s + 1), pick(u, s, links), 6 + s).wait_recv()
-
-    def push_done(u, owner):
-        place = out_ref.at[owner, :, pl.ds(pl.multiple_of(u * LANES, LANES), LANES)]
-        return push(place, place, send.at[9, u], recv.at[9, u], mate)
+        return push(place, place, send.at[k], recv.at[k, u], to)
+
+    def push_gather(u, s, begin, size):
+        return push_rows(u, begin, size, pick(u, s, links), 8 - s)
+
+    def push_done(b):
+        place = out_ref.at[core, :, pl.ds(pl.multiple_of(b * COLS, COLS), COLS)]
+        return push(place, place, send.at[9], done_recv, mate)
 
     def each(begin, count, size, fn):
         step = min(size, count)
@@ -241,7 +238,6 @@
         size = rows >> (s + 1)
         bit = pick(u, s, bits)
         base = kept(u, s) - kept(u, 1)
-        push_half(u, s - 1).wait_recv()
         gone, stay = (1 - bit) * size, bit * size
 
         def at(begin, i, n):
@@ -260,7 +256,6 @@
             ] + inbox[s - 1][u, at(stay, i, n), :].astype(F32)
 
     def scatter(u):
-        push_half(u, 2).wait_recv()
         base = kept(u, 3) - kept(u, 1)
         at = pl.ds(pl.multiple_of(base, PIECE), 8 * PIECE)
         both = keep[u, at, :] + rv2[u].astype(F32)
@@ -270,7 +265,6 @@
         keep[u, at, :] = both
 
     def swap(u):
-        all_cube(u, 3).wait_recv()
         both = keep[u, pl.ds(pl.multiple_of(kept(u, 6) - kept(u, 1), PIECE), PIECE), :]
         for m in range(7):
             both = both + cube_in[u, m].astype(F32)
@@ -278,7 +272,6 @@
         push_far(u).start()
 
     def total(u):
-        push_far(u).wait_recv()
         both = (x_out[u].astype(F32) + x_in[u].astype(F32)).astype(BF16)
         begin = kept(u, 6)
         at = pl.ds(pl.multiple_of(begin, PIECE), PIECE)
@@ -287,42 +280,41 @@
             push_rows(u, begin, PIECE, to, 5).start()
 
     def spread(u):
-        all_cube(u, 5).wait_recv()
-        push_gather(u, 2).start()
+        begin = kept(u, 3)
+        for s in (2, 1, 0):
+            push_gather(u, s, begin, rows >> 3).start()
 
     def gather(u, s):
-        wait_gather(u, s + 1)
-        push_gather(u, s).start()
-
-    def done(u):
-        wait_gather(u, 0)
-        push_done(u, core).start()
+        begin = kept(u, s + 1) + (1 - pick(u, s + 1, bits)) * (rows >> (s + 2))
+        for k in range(s, -1, -1):
+            push_gather(u, k, begin, rows >> (s + 2)).start()
 
     steps = (
-        (DONE, done),
+        (HALVE1, lambda u: halve(u, 1)),
+        (HALVE2, lambda u: halve(u, 2)),
+        (SCATTER, scatter),
+        (SWAP, swap),
+        (SUM, total),
+        (SPREAD, spread),
+        (GATHER1, lambda u: gather(u, 1)),
         (GATHER0, lambda u: gather(u, 0)),
-        (GATHER1, lambda u: gather(u, 1)),
-        (SPREAD, spread),
-        (SUM, total),
-        (SWAP, swap),
-        (SCATTER, scatter),
-        (HALVE2, lambda u: halve(u, 2)),
-        (HALVE1, lambda u: halve(u, 1)),
+        (DONE, None),
     )
 
     def tick(t, part):
-        for delay, fn in steps:
+        for k, (delay, fn) in enumerate(steps):
             if delay % 2 != part:
                 continue
             b = t - delay // 2
 
             @pl.when((b >= 0) & (b < blocks))
-            def _(b=b, fn=fn):
-                def one(h, _):
-                    fn(2 * b + h)
-                    return 0
-
-                lax.fori_loop(0, 2, one, 0)
+            def _(b=b, k=k, fn=fn):
+                for h in range(2):
+                    arrived(2 * b + h, k)
+                    if fn is not None:
+                        fn(2 * b + h)
+                if fn is None:
+                    push_done(b).start()
 
     def slot(t, _):
         @pl.when(t + 1 < blocks)
@@ -347,24 +339,12 @@
 
     lax.fori_loop(0, blocks + DONE // 2, slot, 0)
 
-    def finish_block(b, _):
-        push_mate(b).wait_send()
-        return 0
-
-    lax.fori_loop(0, blocks, finish_block, 0)
-
-    def finish(u, _):
-        for s in range(3):
-            push_half(u, s).wait_send()
-            push_gather(u, s).wait_send()
-        all_cube(u, 3).wait_send()
-        all_cube(u, 5).wait_send()
-        push_far(u).wait_send()
-        push_done(u, 1 - core).wait_recv()
-        push_done(u, core).wait_send()
-        return 0
-
-    lax.fori_loop(0, units, finish, 0)
+    sent = (st0, st1, st2, cube_in, x_out, cube_in, st2, st1, st0, out_ref.at[core])
+    for k, all_of in enumerate(sent):
+        push(all_of, all_of, send.at[k], done_recv, mate).wait_send()
+    push(p_out, p_out, p_send, done_recv, mate).wait_send()
+    whole = out_ref.at[1 - core]
+    push(whole, whole, send.at[9], done_recv, mate).wait_recv()
 
 
 def flush(sums_ref, out_ref, sem):
@@ -411,10 +391,11 @@
                 pltpu.VMEM((units, PIECE, LANES), BF16),
                 dma((2,)),
                 dma((4,)),
+                dma,
                 dma((blocks,)),
-                dma((blocks,)),
-                dma((10, units)),
-                dma((10, units)),
+                dma((10,)),
+                dma((9, units)),
+                dma,
             ],
             compiler_params=pltpu.CompilerParams(
                 collective_id=0, has_side_effects=True, vmem_limit_bytes=46 * 2**20

time: 105 us -> 94.6 us (0.901)
  Pallas kernels: 105 us -> 94.5 us
    pallas_call x1, Pallas kernels: 101 us -> 90.2 us  [step(): pl.pallas_call(functools.partial(kernel, blocks), out_shape=pltpu.VMEM((n...]
where the time goes in v3:
time: 94.6 us; the launch traced here: 94.5 us
  Pallas kernels  94.5 us (100%)
    pallas_call x1, Pallas kernels, step(): pl.pallas_call(functools.partial(kernel, blocks), out_shape=pltpu.VMEM((n...  90.2 us
    pallas_call x1, Pallas kernels, step(): pl.pallas_call(flush, out_shape=jax.ShapeDtypeStruct((n, d, f), BF16), in...  4.33 us

profile of v3, /device:TPU:1, one launch (start us, length us, event | category | flops | bytes accessed | tf_op | source)
XLA Modules:
  0.0 94.5 jit_solution(14200932624712454692)
XLA Ops:
  0.0 90.2 %sums.1.sums_ref = bf16[2,1024,2816]{2,1,0:T(8,128)(2,1)S(1)} custom-call(bf16[1,2,2048,1024]{3,2,1,0:T(8,128)(2,1)} %a_ref.1, bf16[1,2,2048,2816]{3,2,1,0:T(8,128)(2,1)} %g_ref.1), custom_call_target="tpu_custom_call" | custom-call | tf_op jit(solution)/shard_map/sums/pallas_call | solution.py:374
  90.2 4.3 %flush.1 = bf16[2,1024,2816]{2,1,0:T(8,128)(2,1)} custom-call(bf16[2,1024,2816]{2,1,0:T(8,128)(2,1)S(1)} %sums.1.sums_ref), custom_call_target="tpu_custom_call" | custom-call | tf_op jit(solution)/shard_map/flush/pallas_call | solution.py:405

commit v4 on v3

--- a/solution.py
+++ b/solution.py
@@ -11,8 +11,8 @@
 COLS = 256
 LANES = 128
 PIECE = 16
-HALVE1, HALVE2, SCATTER, SWAP, SUM = 4, 7, 11, 15, 21
-SPREAD, GATHER1, GATHER0, DONE = 26, 31, 37, 45
+HALVE1, HALVE2, SCATTER, SWAP, SUM = 5, 9, 13, 18, 24
+SPREAD, GATHER1, GATHER0, DONE = 30, 35, 41, 48
 
 
 def kernel(
@@ -309,10 +309,13 @@
 
             @pl.when((b >= 0) & (b < blocks))
             def _(b=b, k=k, fn=fn):
-                for h in range(2):
+                def one(h, _):
                     arrived(2 * b + h, k)
                     if fn is not None:
                         fn(2 * b + h)
+                    return 0
+
+                lax.fori_loop(0, 2, one, 0)
                 if fn is None:
                     push_done(b).start()
 

time: 94.6 us -> 92.9 us (0.982)
  Pallas kernels: 94.5 us -> 92.8 us
    pallas_call x1, Pallas kernels: 90.2 us -> 88.5 us  [step(): pl.pallas_call(functools.partial(kernel, blocks), out_shape=pltpu.VMEM((n...]
where the time goes in v4:
time: 92.9 us; the launch traced here: 92.8 us
  Pallas kernels  92.8 us (100%)
    pallas_call x1, Pallas kernels, step(): pl.pallas_call(functools.partial(kernel, blocks), out_shape=pltpu.VMEM((n...  88.5 us
    pallas_call x1, Pallas kernels, step(): pl.pallas_call(flush, out_shape=jax.ShapeDtypeStruct((n, d, f), BF16), in...  4.33 us

profile of v4, /device:TPU:1, one launch (start us, length us, event | category | flops | bytes accessed | tf_op | source)
XLA Modules:
  0.0 92.8 jit_solution(11890866568200687599)
XLA Ops:
  0.0 88.5 %sums.1.sums_ref = bf16[2,1024,2816]{2,1,0:T(8,128)(2,1)S(1)} custom-call(bf16[1,2,2048,1024]{3,2,1,0:T(8,128)(2,1)} %a_ref.1, bf16[1,2,2048,2816]{3,2,1,0:T(8,128)(2,1)} %g_ref.1), custom_call_target="tpu_custom_call" | custom-call | tf_op jit(solution)/shard_map/sums/pallas_call | solution.py:377
  88.5 4.3 %flush.1 = bf16[2,1024,2816]{2,1,0:T(8,128)(2,1)} custom-call(bf16[2,1024,2816]{2,1,0:T(8,128)(2,1)S(1)} %sums.1.sums_ref), custom_call_target="tpu_custom_call" | custom-call | tf_op jit(solution)/shard_map/flush/pallas_call | solution.py:408
